TPU v7x, 32 devices: a whole 2x2x4 slice. The times are simulated.
32 devices in a mesh: gx: 4 (over z), gy: 2 (over y), gz: 4 (over x, core).
Axes of the slice: x: 2, y: 2, z: 4, core: 2. Of those that a mesh axis runs over, the one named last changes fastest.
Arguments:
- colloc: bfloat16 [768, 4000], P(('gx', 'gy')), may hold values from -6 to 6
- occ_coeffs: bfloat16 [4000, 1024], P(None, 'gz'), may hold values from -0.09375 to 0.09375
- core: bfloat16 [768, 2, 384], P('gx', 'gy'), may hold values from -6.246567e-05 to 6.246567e-05
Outputs:
- coulomb: float32 [96, 4000], P(('gx', 'gz'), 'gy')
- exchange: float32 [96, 4000], P(('gx', 'gz'), 'gy')
All inputs are finite; a program needn't handle non-finite values.
Results may differ from a plain program's by a relative error of at most 0.0089.
Values may be sent and summed in bfloat16 or wider, within the bound.
A program may use at most 64 MiB of HBM per device.

v0:
```python
import functools

import jax
import jax.numpy as jnp
import numpy as np
from jax import lax
from jax.experimental import pallas as pl
from jax.experimental.pallas import tpu as pltpu
from jax.sharding import PartitionSpec as P

W = 96
LANES = 128
DEPTH = 1024
MESH = pl.DeviceIdType.MESH
F32 = jnp.float32
BF16 = jnp.bfloat16


def up(value, step):
    return -(-value // step) * step


def dot(left, right, left_dim, right_dim):
    return lax.dot_general(
        left, right, (((left_dim,), (right_dim,)), ((), ())), preferred_element_type=F32
    )


def kernel(
    dims,
    colloc_hbm,
    coeffs_hbm,
    core_hbm,
    place_hbm,
    out_ref,
    vals,
    coeffs,
    core,
    place,
    core_q,
    row_occ,
    col_occ,
    col_win,
    win_t,
    dens,
    stage,
    cols,
    pot_send,
    pot_recv,
    tot_send,
    tot_recv,
    z_send,
    z_recv,
    load_sem,
    depth_sem,
    ready,
    known,
    row_sem,
    col_sem,
    col_win_sem,
    dens_sem,
    cols_sem,
    pot_sem,
    tot_sem,
    z_sem,
):
    gx_size, gy_size, gz_size, rows, width = dims
    gx, gy, gz = lax.axis_index("gx"), lax.axis_index("gy"), lax.axis_index("gz")
    points, total = vals.shape
    lanes = col_win.shape[2]
    crowd = gy_size * gz_size
    halves = 2 if gz_size % 2 == 0 else 1
    half = points // halves
    base = gz - lax.rem(gz, halves)
    span = cols.shape[2]
    side = gy_size * points
    part = lax.rem(gz, halves)

    def turn(pos, step, size):
        if size & (size - 1):
            return lax.rem(pos + step, size) if step else pos
        bit = 1
        while bit <= step:
            if step & bit:
                pos = pos + bit * (1 - 2 * lax.rem(lax.div(pos, bit), 2))
            bit *= 2
        return pos

    planes = [turn(gx, d, gx_size) for d in range(1, gx_size)]
    sides = [turn(gy, d, gy_size) for d in range(1, gy_size)]
    flat = [
        (turn(gy, dy, gy_size), turn(gz, dz, gz_size))
        for dy in range(gy_size)
        for dz in range(gz_size)
        if dy or dz
    ]
    mine = gy * gz_size + gz
    own = gy * halves + part
    mate = (gx, gy, turn(gz, 1, gz_size))

    def copy(src, dst, sems, target, slot=0):
        return pltpu.make_async_remote_copy(
            src_ref=src,
            dst_ref=dst,
            send_sem=sems.at[0],
            recv_sem=sems.at[1 + slot],
            device_id=target,
            device_id_type=MESH,
        )

    def arrive(ref, sems, slot=0):
        copy(ref, ref, sems, mate, slot).wait_recv()

    def leave(ref, sems):
        copy(ref, ref, sems, mate).wait_send()

    def seat(i):
        return lax.div(i, gz_size), lax.rem(i, gz_size)

    def sweep(body):
        if crowd <= 16:
            for i in range(crowd):
                body(jnp.int32(i))
        else:
            lax.fori_loop(0, crowd, lambda i, c: (body(i), c)[1], 0)

    own_rows = pl.ds(pl.multiple_of(part * half, half), half)

    def col_win_copy(h):
        return copy(vals.at[:, pl.ds(0, lanes)], col_win.at[gy], col_win_sem, (gx, h, gz))

    def dens_copy(t):
        some = dens.at[gx]
        return copy(some, some, dens_sem, (t, gy, gz))

    def row_copy(t, k):
        src = col_occ.at[own, pl.ds(k * half, half)]
        return copy(src, row_occ.at[gx * halves + part], row_sem, (t, gy, base + k), gx)

    def col_copy(h):
        some = col_occ.at[own]
        return copy(some, some, col_sem, (gx, h, gz))

    def col_fwd(h):
        some = col_occ.at[h * halves + part]
        return copy(some, some, col_sem, mate, 1)

    def cols_copy(h):
        at = pl.ds(pl.multiple_of(part * half, half), half)
        return copy(stage.at[h, at], cols.at[gy, at], cols_sem, (gx, h, gz))

    def cols_fwd(h):
        some = cols.at[h, pl.ds(pl.multiple_of(part * half, half), half)]
        return copy(some, some, cols_sem, mate, 1)

    def pot_copy(h, g):
        return copy(pot_send, pot_recv.at[mine], pot_sem, (gx, h, g))

    def tot_copy(t, h, g):
        return copy(tot_send.at[t, g], tot_recv.at[gx * crowd + mine], tot_sem, (t, h, g))

    def z_copy(index, t):
        return copy(z_send.at[index, t], z_recv.at[index, gx], z_sem, (t, gy, gz), index)

    load_core = pltpu.make_async_copy(core_hbm, core, load_sem.at[0])
    load_vals = pltpu.make_async_copy(colloc_hbm, vals, load_sem.at[1])
    load_place = pltpu.make_async_copy(place_hbm, place, load_sem.at[2])
    spans = [(s, min(DEPTH, total - s)) for s in range(0, total, DEPTH)]
    depth_loads = [
        pltpu.make_async_copy(
            coeffs_hbm.at[pl.ds(s, n)], coeffs.at[pl.ds(s, n)], depth_sem.at[i]
        )
        for i, (s, n) in enumerate(spans)
    ]
    load_vals.start()
    for load in depth_loads:
        load.start()
    load_core.start()
    load_place.start()

    barrier = pltpu.get_barrier_semaphore()
    def greet(sem, before):
        for t in range(gx_size):
            for g in range(gz_size):
                ahead = gx > t if before else gx < t

                @pl.when(ahead)
                def _():
                    pl.semaphore_signal(sem, inc=1, device_id=(t, gy, g), device_id_type=MESH)

        def inside(i):
            @pl.when(i < mine if before else i > mine)
            def _():
                pl.semaphore_signal(sem, inc=1, device_id=(gx, *seat(i)), device_id_type=MESH)

        sweep(inside)

    greet(barrier, False)

    @pl.when(gx * gz_size + mine > 0)
    def _():
        pl.semaphore_wait(barrier, gx * gz_size + mine)

    greet(ready.at[gx], True)

    def contract(first, last):
        acc = jnp.zeros((points, coeffs.shape[1]), F32)
        for i in range(first, last):
            s, n = spans[i]
            depth_loads[i].wait()
            acc += dot(vals[:, s : s + n], coeffs[s : s + n, :], 1, 0)
        return acc

    load_vals.wait()
    occ = contract(0, len(spans))
    occ = occ.astype(BF16)
    col_occ[own] = occ
    square = jnp.square(occ.astype(F32))
    high = square.astype(BF16)
    low = (square - high.astype(F32)).astype(BF16)
    ones = jnp.ones((8, occ.shape[1]), BF16)
    dens[gx] = (dot(ones, high, 1, 1) + dot(ones, low, 1, 1))[:1]
    for t in range(gx_size - 1):

        @pl.when(gx > t)
        def _():
            dens_copy(t).start()
            for k in range(halves):
                row_copy(t, k).start()


    @pl.when(mine < crowd - 1)
    def _():
        pl.semaphore_wait(ready.at[gx], crowd - 1 - mine)

    for h in sides:
        col_copy(h).start()
    if halves > 1:
        col_fwd(gy).start()
    for h in sides:
        col_win_copy(h).start()
    for h in range(gy_size):
        stage[h, :, :width] = vals[:, h * width : (h + 1) * width]
        if width < span:
            stage[h, :, width:] = jnp.zeros((points, span - width), BF16)
    for h in sides:
        cols_copy(h).start()
    own_cols = pltpu.make_async_copy(stage.at[gy], cols.at[gy], load_sem.at[3])
    own_cols.start()
    for t in range(1, gx_size):

        @pl.when(gx < t)
        def _():
            pl.semaphore_wait(ready.at[t], gz_size)
            dens_copy(t).start()
            for k in range(halves):
                row_copy(t, k).start()

    for h in sides:
        pl.semaphore_signal(known, inc=1, device_id=(gx, h, gz), device_id_type=MESH)
    col_win[gy] = vals[:, :lanes]
    load_core.wait()
    load_place.wait()
    spread = place[...]
    for k in range(halves):

        @pl.when(part == k)
        def _():
            starts = [a * points + k * half for a in range(gx_size)]
            core_q[...] = jnp.concatenate([core[:, s : s + half] for s in starts], axis=1)

    if sides:
        arrive(col_occ.at[pl.ds(0, len(sides))], col_sem)
    if halves > 1:
        for h in sides:
            col_fwd(h).start()
    if planes:
        arrive(dens.at[pl.ds(0, len(planes))], dens_sem)
    density = jnp.concatenate([dens[z] for z in range(gx_size)], axis=1)
    density = jnp.broadcast_to(density, (8, core.shape[1])).astype(BF16)
    potential = dot(density, core[...], 1, 1)[:1]
    pot_send[...] = potential
    for h, g in flat:
        pot_copy(h, g).start()

    if sides:
        arrive(col_win.at[pl.ds(0, len(sides))], col_win_sem)
    wins = dot(spread, col_win[...].reshape(side, lanes), 0, 1)
    win_t[...] = wins.reshape(win_t.shape)
    win_rows = wins.astype(BF16)

    if halves > 1:
        arrive(col_occ.at[pl.ds(0, gy_size)], col_sem, 1)
    for k in range(halves):
        row_occ[gx * halves + k] = col_occ[gy * halves + k, own_rows]
    for z in planes:
        arrive(row_occ.at[pl.ds(z * halves, halves)], row_sem, z)
    gram = None
    for k in range(halves):
        row_vals = [row_occ[z * halves + k] for z in range(gx_size)]
        col_vals = [col_occ[h * halves + k] for h in range(gy_size)]
        row_vals, col_vals = (jnp.concatenate(v, axis=0) for v in (row_vals, col_vals))
        term = dot(col_vals, row_vals, 1, 1)
        gram = term if gram is None else gram + term
    mixed = (core_q[...].astype(F32) * gram).astype(BF16)
    block = dot(win_rows, mixed, 1, 0)
    tight = win_t.shape[1]
    layers = tight // 8
    bands = []
    for j in range(layers):
        starts = [g * tight + j * 8 for g in range(gz_size)]
        bands.append(jnp.concatenate([block[at : at + 8] for at in starts], axis=0))
    for z in range(gx_size):
        pack = [band[:, z * half : (z + 1) * half] for band in bands]
        pack = jnp.concatenate(pack, axis=1).reshape(tot_send.shape[1:])
        tot_send[z] = pack.astype(BF16)
    if gy_size > 1:
        pl.semaphore_wait(known, gy_size - 1)
    for t in planes[::-1]:
        sweep(lambda i: tot_copy(t, *seat(i)).start())
    for h, g in flat:
        tot_copy(gx, h, g).start()
    own_tot = pltpu.make_async_copy(
        tot_send.at[gx, gz], tot_recv.at[gx * crowd + mine], tot_sem.at[1]
    )
    own_tot.start()

    if sides:
        arrive(cols.at[pl.ds(0, len(sides)), pl.ds(0, half)], cols_sem)
    if halves > 1:
        for h in sides:
            cols_fwd(h).start()

    spare = 8 - rows
    reach = z_send.shape[3]
    tail = span - reach

    def spread_out(index, left):
        gap = jnp.zeros((spare, side), F32)
        lines = []
        for a in range(gx_size):
            lines += [left[a * rows : (a + 1) * rows], gap]
        lefts = jnp.concatenate(lines, axis=0).astype(BF16)
        out = dot(lefts, cols[...].reshape(side, span), 1, 0).reshape(gx_size, 8, span)
        line = lax.broadcasted_iota(jnp.int32, (8, tail), 0)
        for a in range(gx_size):
            for j in range(reach // tail):
                block = out[a, :, j * tail : (j + 1) * tail]
                if j * spare < rows:
                    moved = pltpu.roll(out[a, :, reach:], (rows - j * spare) % 8, 0)
                    block = jnp.where(line < rows, block, moved)
                z_send[index, a, :, j * tail : (j + 1) * tail] = block.astype(BF16)
            if reach % tail:
                at = reach // tail * tail
                z_send[index, a, :, at:] = out[a, :, at:reach].astype(BF16)
        for t in planes[::-1]:
            z_copy(index, t).start()

    if flat:
        arrive(pot_recv.at[pl.ds(0, len(flat))], pot_sem)
    pot = pot_send[...]
    for h, g in flat:
        pot += pot_recv[h * gz_size + g]
    weighted = (win_t[gz] * pot).astype(BF16).astype(F32)
    own_cols.wait()
    if halves > 1 and sides:
        arrive(cols.at[pl.ds(0, len(sides)), pl.ds(0, half)], cols_sem, 1)
    spread_out(0, weighted)

    arrive(tot_recv, tot_sem)
    total_of = []
    for i in range(gy_size * halves):
        h, k = divmod(i, halves)
        slots = [
            z * crowd + h * gz_size + g
            for z in range(gx_size)
            for g in range(k, gz_size, halves)
        ]
        total_of.append(sum(tot_recv[slot].astype(F32) for slot in slots))
    owned = [
        jnp.concatenate([one[:, j * half : (j + 1) * half] for one in total_of], axis=1)
        for j in range(layers)
    ]
    owned = jnp.concatenate(owned, axis=0)
    spread_out(1, owned)

    if sides:
        leave(col_win.at[pl.ds(0, len(sides))], col_win_sem)
        leave(cols.at[pl.ds(0, len(sides))], cols_sem)
    if planes:
        leave(dens.at[pl.ds(0, len(planes))], dens_sem)
        leave(row_occ.at[pl.ds(0, len(planes) * halves)], row_sem)
    leave(col_occ.at[pl.ds(0, len(sides) + gy_size * (halves - 1))], col_sem)
    leave(pot_recv.at[pl.ds(0, len(flat))], pot_sem)
    leave(tot_recv.at[pl.ds(0, gx_size * crowd - 1)], tot_sem)

    for index in range(2):
        if planes:
            arrive(z_recv.at[index, pl.ds(0, len(planes))], z_sem, index)
        acc = z_send[index, gx].astype(F32)
        for z in planes:
            acc += z_recv[index, z].astype(F32)
        out_ref[index, :, :reach] = acc[:rows]
        for r in range(rows):
            j, k = divmod(r, spare)
            line = acc[rows + k : rows + k + 1, j * tail : j * tail + width - reach]
            out_ref[index, r : r + 1, reach:] = line

    if planes:
        leave(z_recv.at[:, pl.ds(0, len(planes))], z_sem)


def local(colloc, occ_coeffs, core):
    points, total = colloc.shape
    gx_size = lax.axis_size("gx")
    gy_size = lax.axis_size("gy")
    gz_size = lax.axis_size("gz")
    occupied = occ_coeffs.shape[1]
    rows = W // (gx_size * gz_size)
    width = total // gy_size
    row_count, flat = core.shape[0], core.shape[2]
    lanes = up(W, LANES)
    side = gy_size * points
    span = up(width, LANES)
    halves = 2 if gz_size % 2 == 0 else 1
    half = points // halves
    tiles = span // LANES
    spare = 8 - rows
    tail = max(t for t in range(1, tiles) if (tiles - t) // t * spare >= rows)
    reach = span - tail * LANES

    used = gx_size * rows
    tight = up(used, 8)
    place = np.zeros((lanes, gz_size, tight), np.float32)
    for a in range(gx_size):
        for g in range(gz_size):
            for k in range(rows):
                place[(a * gz_size + g) * rows + k, g, a * rows + k] = 1
    place = jnp.asarray(place.reshape(lanes, gz_size * tight), BF16)

    dims = (gx_size, gy_size, gz_size, rows, width)
    dma = pltpu.SemaphoreType.DMA
    vmem = pltpu.VMEM
    result = pl.pallas_call(
        functools.partial(kernel, dims),
        out_shape=pltpu.VMEM((2, rows, width), F32),
        in_specs=[pl.BlockSpec(memory_space=pltpu.HBM)] * 4,
        out_specs=pl.BlockSpec(memory_space=pltpu.VMEM),
        scratch_shapes=[
            vmem((points, total), BF16),
            vmem((total, occupied), BF16),
            vmem((row_count, flat), BF16),
            vmem(place.shape, BF16),
            vmem((row_count, gx_size * half), BF16),
            vmem((gx_size * halves, half, occupied), BF16),
            vmem((gy_size * halves, points, occupied), BF16),
            vmem((gy_size, points, lanes), BF16),
            vmem((gz_size, tight, side), F32),
            vmem((gx_size, 1, points), F32),
            vmem((gy_size, points, span), BF16),
            vmem((gy_size, points, span), BF16),
            vmem((1, side), F32),
            vmem((gy_size * gz_size, 1, side), F32),
            vmem((gx_size, gz_size, 8, tight // 8 * half), BF16),
            vmem((gx_size * gy_size * gz_size, 8, tight // 8 * half), BF16),
            vmem((2, gx_size, 8, reach), BF16),
            vmem((2, gx_size, 8, reach), BF16),
            dma((4,)),
            dma((-(-total // DEPTH),)),
            pltpu.SemaphoreType.REGULAR((gx_size,)),
            pltpu.SemaphoreType.REGULAR,
            dma((1 + gx_size,)),
            dma((3,)),
            dma((2,)),
            dma((2,)),
            dma((3,)),
            dma((2,)),
            dma((2,)),
            dma((3,)),
        ],
        compiler_params=pltpu.CompilerParams(
            collective_id=0, has_side_effects=True, vmem_limit_bytes=60 * 1024 * 1024
        ),
    )(colloc, occ_coeffs, core.reshape(row_count, flat), place)
    return result[0], result[1]


def solution(mesh):
    in_specs = (P(("gx", "gy"), None), P(None, "gz"), P("gx", "gy", None))
    out_specs = (P(("gx", "gz"), "gy"), P(("gx", "gz"), "gy"))
    return jax.shard_map(local, mesh=mesh, in_specs=in_specs, out_specs=out_specs, check_vma=False)
```

profile of v0, /device:TPU:0, one launch (start us, length us, event | category | flops | bytes accessed | tf_op | source)
XLA Modules:
  0.0 23.9 jit_solution(13833703538727514655)
XLA Ops:
  0.6 22.6 %shard_map.59 = f32[2,6,2000]{2,1,0:T(8,128)S(1)} custom-call(bf16[96,4000]{1,0:T(8,128)(2,1)} %colloc_hbm.1, bf16[4000,256]{1,0:T(8,128)(2,1)} %coeffs_hbm.1, bf16[192,384]{1,0:T(8,128)(2,1)} %bitcast.5, bf16[128,96]{1,0:T(8,128)(2,1)} %constant.2.clone.place_hbm), custom_call_target="tpu_custom_call" | custom-call | tf_op jit(solution)/shard_map/pallas_call | solution.py:444
  23.2 0.7 %slice_bitcast_fusion = (f32[6,2000]{1,0:T(8,128)}, f32[6,2000]{1,0:T(8,128)}) fusion(f32[2,6,2000]{2,1,0:T(8,128)S(1)} %shard_map.59), kind=kLoop, calls=%fused_computation | loop fusion | bytes 192000 | tf_op jit(solution)/shard_map/squeeze | solution.py:485
where the time goes:
time: 24 us; the launch traced here: 23.9 us
  Pallas kernels  22.6 us (94%)
  local copies, waits for them, and re-layouts  0.66 us (3%)
  between operations  0.64 us (3%)
    pallas_call x1, Pallas kernels, local(): pl.pallas_call(functools.partial(kernel, dims), out_shape=pltpu.VMEM((2,...  22.6 us
    squeeze x1, local copies, waits for them, and re-layouts, local(): return (result[0], result[1])  0.66 us

commit v1 on v0

--- a/solution.py
+++ b/solution.py
@@ -96,7 +96,13 @@
     ]
     mine = gy * gz_size + gz
     own = gy * halves + part
-    mate = (gx, gy, turn(gz, 1, gz_size))
+    mate = (gx, gy, base + halves - 1 - part)
+    same = [
+        (turn(gy, dy, gy_size), turn(gz, dz, gz_size))
+        for dy in range(gy_size)
+        for dz in range(0, gz_size, halves)
+        if dy or dz
+    ]
 
     def copy(src, dst, sems, target, slot=0):
         return pltpu.make_async_remote_copy(
@@ -173,33 +179,37 @@
         for i, (s, n) in enumerate(spans)
     ]
     load_vals.start()
-    for load in depth_loads:
+    depth_loads[0].start()
+
+    barrier = pltpu.get_barrier_semaphore()
+    def greet(sem, before):
+        for t in range(gx_size):
+
+            @pl.when(gx > t if before else gx < t)
+            def _():
+                for k in range(halves):
+                    pl.semaphore_signal(
+                        sem, inc=1, device_id=(t, gy, base + k), device_id_type=MESH
+                    )
+
+        for h, g in same + [mate[1:]] * (halves - 1):
+            i = h * gz_size + g
+
+            @pl.when(i < mine if before else i > mine)
+            def _():
+                pl.semaphore_signal(sem, inc=1, device_id=(gx, h, g), device_id_type=MESH)
+
+    greet(barrier, False)
+    for load in depth_loads[1:]:
         load.start()
     load_core.start()
     load_place.start()
-
-    barrier = pltpu.get_barrier_semaphore()
-    def greet(sem, before):
-        for t in range(gx_size):
-            for g in range(gz_size):
-                ahead = gx > t if before else gx < t
-
-                @pl.when(ahead)
-                def _():
-                    pl.semaphore_signal(sem, inc=1, device_id=(t, gy, g), device_id_type=MESH)
-
-        def inside(i):
-            @pl.when(i < mine if before else i > mine)
-            def _():
-                pl.semaphore_signal(sem, inc=1, device_id=(gx, *seat(i)), device_id_type=MESH)
-
-        sweep(inside)
-
-    greet(barrier, False)
-
-    @pl.when(gx * gz_size + mine > 0)
+    below = lax.div(mine, halves) + part
+    above = crowd // halves + halves - 2 - below
+
+    @pl.when(gx + below > 0)
     def _():
-        pl.semaphore_wait(barrier, gx * gz_size + mine)
+        pl.semaphore_wait(barrier, gx * halves + below)
 
     greet(ready.at[gx], True)
 
@@ -229,9 +239,9 @@
                 row_copy(t, k).start()
 
 
-    @pl.when(mine < crowd - 1)
+    @pl.when(above > 0)
     def _():
-        pl.semaphore_wait(ready.at[gx], crowd - 1 - mine)
+        pl.semaphore_wait(ready.at[gx], above)
 
     for h in sides:
         col_copy(h).start()
@@ -251,13 +261,13 @@
 
         @pl.when(gx < t)
         def _():
-            pl.semaphore_wait(ready.at[t], gz_size)
+            pl.semaphore_wait(ready.at[t], halves)
             dens_copy(t).start()
             for k in range(halves):
                 row_copy(t, k).start()
 
-    for h in sides:
-        pl.semaphore_signal(known, inc=1, device_id=(gx, h, gz), device_id_type=MESH)
+    for h, g in same:
+        pl.semaphore_signal(known, inc=1, device_id=(gx, h, g), device_id_type=MESH)
     col_win[gy] = vals[:, :lanes]
     load_core.wait()
     load_place.wait()
@@ -280,6 +290,8 @@
     density = jnp.broadcast_to(density, (8, core.shape[1])).astype(BF16)
     potential = dot(density, core[...], 1, 1)[:1]
     pot_send[...] = potential
+    if same:
+        pl.semaphore_wait(known, len(same))
     for h, g in flat:
         pot_copy(h, g).start()
 
@@ -310,16 +322,20 @@
     for j in range(layers):
         starts = [g * tight + j * 8 for g in range(gz_size)]
         bands.append(jnp.concatenate([block[at : at + 8] for at in starts], axis=0))
-    for z in range(gx_size):
+    for z in reversed(range(gx_size)):
         pack = [band[:, z * half : (z + 1) * half] for band in bands]
         pack = jnp.concatenate(pack, axis=1).reshape(tot_send.shape[1:])
         tot_send[z] = pack.astype(BF16)
-    if gy_size > 1:
-        pl.semaphore_wait(known, gy_size - 1)
-    for t in planes[::-1]:
-        sweep(lambda i: tot_copy(t, *seat(i)).start())
-    for h, g in flat:
-        tot_copy(gx, h, g).start()
+
+        @pl.when(gx != z)
+        def _():
+            sweep(lambda i: tot_copy(z, *seat(i)).start())
+
+        @pl.when(gx == z)
+        def _():
+            for h, g in flat:
+                tot_copy(z, h, g).start()
+
     own_tot = pltpu.make_async_copy(
         tot_send.at[gx, gz], tot_recv.at[gx * crowd + mine], tot_sem.at[1]
     )
@@ -353,8 +369,11 @@
             if reach % tail:
                 at = reach // tail * tail
                 z_send[index, a, :, at:] = out[a, :, at:reach].astype(BF16)
-        for t in planes[::-1]:
-            z_copy(index, t).start()
+        for t in range(gx_size):
+
+            @pl.when(gx != t)
+            def _():
+                z_copy(index, t).start()
 
     if flat:
         arrive(pot_recv.at[pl.ds(0, len(flat))], pot_sem)

time: 24 us -> 23.9 us (level)
  no operation moved by 1% of the time
where the time goes in v1:
time: 23.9 us; the launch traced here: 23.8 us
  Pallas kernels  22.5 us (94%)
  local copies, waits for them, and re-layouts  0.66 us (3%)
  between operations  0.64 us (3%)
    pallas_call x1, Pallas kernels, local(): pl.pallas_call(functools.partial(kernel, dims), out_shape=pltpu.VMEM((2,...  22.5 us
    squeeze x1, local copies, waits for them, and re-layouts, local(): return (result[0], result[1])  0.66 us

profile of v1, /device:TPU:0, one launch (start us, length us, event | category | flops | bytes accessed | tf_op | source)
XLA Modules:
  0.0 23.8 jit_solution(7337971508088888475)
XLA Ops:
  0.6 22.5 %shard_map.59 = f32[2,6,2000]{2,1,0:T(8,128)S(1)} custom-call(bf16[96,4000]{1,0:T(8,128)(2,1)} %colloc_hbm.1, bf16[4000,256]{1,0:T(8,128)(2,1)} %coeffs_hbm.1, bf16[192,384]{1,0:T(8,128)(2,1)} %bitcast.5, bf16[128,96]{1,0:T(8,128)(2,1)} %constant.2.clone.place_hbm), custom_call_target="tpu_custom_call" | custom-call | tf_op jit(solution)/shard_map/pallas_call | solution.py:463
  23.1 0.7 %slice_bitcast_fusion = (f32[6,2000]{1,0:T(8,128)}, f32[6,2000]{1,0:T(8,128)}) fusion(f32[2,6,2000]{2,1,0:T(8,128)S(1)} %shard_map.59), kind=kLoop, calls=%fused_computation | loop fusion | bytes 192000 | tf_op jit(solution)/shard_map/squeeze | solution.py:504

commit v2 on v1

--- a/solution.py
+++ b/solution.py
@@ -38,6 +38,10 @@
     core,
     place,
     core_q,
+    cores,
+    core_t,
+    row_win,
+    back,
     row_occ,
     col_occ,
     col_win,
@@ -49,6 +53,8 @@
     pot_recv,
     tot_send,
     tot_recv,
+    back_send,
+    back_recv,
     z_send,
     z_recv,
     load_sem,
@@ -56,12 +62,16 @@
     ready,
     known,
     row_sem,
+    core_sem,
+    row_win_sem,
     col_sem,
     col_win_sem,
     dens_sem,
     cols_sem,
+    cols_fwd_sem,
     pot_sem,
     tot_sem,
+    back_sem,
     z_sem,
 ):
     gx_size, gy_size, gz_size, rows, width = dims
@@ -94,6 +104,7 @@
         for dz in range(gz_size)
         if dy or dz
     ]
+    across = [(gy, base + k) for k in range(halves)] + [(h, gz) for h in sides]
     mine = gy * gz_size + gz
     own = gy * halves + part
     mate = (gx, gy, base + halves - 1 - part)
@@ -120,6 +131,52 @@
     def leave(ref, sems):
         copy(ref, ref, sems, mate).wait_send()
 
+    def lane_copy(src, dst, sems, t, target):
+        return pltpu.make_async_remote_copy(
+            src_ref=src,
+            dst_ref=dst,
+            send_sem=sems.at[0, t],
+            recv_sem=sems.at[1, gx],
+            device_id=target,
+            device_id_type=MESH,
+        )
+
+    def lane_wait(ref, sems, z):
+        pltpu.make_async_remote_copy(
+            src_ref=ref,
+            dst_ref=ref,
+            send_sem=sems.at[0, z],
+            recv_sem=sems.at[1, z],
+            device_id=mate,
+            device_id_type=MESH,
+        ).wait_recv()
+
+    def lane_leave(ref, sems, t):
+        pltpu.make_async_remote_copy(
+            src_ref=ref,
+            dst_ref=ref,
+            send_sem=sems.at[0, t],
+            recv_sem=sems.at[1, t],
+            device_id=mate,
+            device_id_type=MESH,
+        ).wait_send()
+
+    steps = range(1, gx_size)
+
+    def other(d):
+        return gx + d if d % 2 else gx - d
+
+    def keeper(d):
+        return gx - d if d % 2 else gx + d
+
+    def inside(t):
+        return (t >= 0) & (t < gx_size)
+
+    def kept_by(z):
+        gap = gx - z
+        odd = lax.rem(jnp.abs(gap), 2)
+        return ((gap > 0) & (odd == 1)) | ((gap < 0) & (odd == 0))
+
     def seat(i):
         return lax.div(i, gz_size), lax.rem(i, gz_size)
 
@@ -141,7 +198,20 @@
 
     def row_copy(t, k):
         src = col_occ.at[own, pl.ds(k * half, half)]
-        return copy(src, row_occ.at[gx * halves + part], row_sem, (t, gy, base + k), gx)
+        return lane_copy(src, row_occ.at[gx * halves + part], row_sem, t, (t, gy, base + k))
+
+    def core_copy(t, h):
+        src = cores.at[t, pl.ds(pl.multiple_of(h * points + part * half, half), half)]
+        return lane_copy(src, core_t.at[gx, gy], core_sem, t, (t, h, gz))
+
+    def row_win_copy(t):
+        src = vals.at[own_rows, pl.ds(0, lanes)]
+        return lane_copy(src, row_win.at[gx], row_win_sem, t, (t, gy, gz))
+
+    def lend(t):
+        row_win_copy(t).start()
+        for h in range(gy_size):
+            core_copy(t, h).start()
 
     def col_copy(h):
         some = col_occ.at[own]
@@ -152,18 +222,21 @@
         return copy(some, some, col_sem, mate, 1)
 
     def cols_copy(h):
-        at = pl.ds(pl.multiple_of(part * half, half), half)
-        return copy(stage.at[h, at], cols.at[gy, at], cols_sem, (gx, h, gz))
+        return copy(stage.at[h], cols.at[gy], cols_sem, (gx, h, gz))
 
     def cols_fwd(h):
-        some = cols.at[h, pl.ds(pl.multiple_of(part * half, half), half)]
-        return copy(some, some, cols_sem, mate, 1)
+        some = cols.at[h]
+        return copy(some, some, cols_fwd_sem, mate)
 
     def pot_copy(h, g):
         return copy(pot_send, pot_recv.at[mine], pot_sem, (gx, h, g))
 
     def tot_copy(t, h, g):
-        return copy(tot_send.at[t, g], tot_recv.at[gx * crowd + mine], tot_sem, (t, h, g))
+        dst = tot_recv.at[gx * crowd + mine]
+        return lane_copy(tot_send.at[t, g], dst, tot_sem, t, (t, h, g))
+
+    def back_copy(h, g):
+        return copy(back_send.at[g], back_recv.at[mine], back_sem, (gx, h, g))
 
     def z_copy(index, t):
         return copy(z_send.at[index, t], z_recv.at[index, gx], z_sem, (t, gy, gz), index)
@@ -178,6 +251,7 @@
         )
         for i, (s, n) in enumerate(spans)
     ]
+    load_core.start()
     load_vals.start()
     depth_loads[0].start()
 
@@ -187,10 +261,8 @@
 
             @pl.when(gx > t if before else gx < t)
             def _():
-                for k in range(halves):
-                    pl.semaphore_signal(
-                        sem, inc=1, device_id=(t, gy, base + k), device_id_type=MESH
-                    )
+                for h, g in across:
+                    pl.semaphore_signal(sem, inc=1, device_id=(t, h, g), device_id_type=MESH)
 
         for h, g in same + [mate[1:]] * (halves - 1):
             i = h * gz_size + g
@@ -202,14 +274,13 @@
     greet(barrier, False)
     for load in depth_loads[1:]:
         load.start()
-    load_core.start()
     load_place.start()
     below = lax.div(mine, halves) + part
     above = crowd // halves + halves - 2 - below
 
     @pl.when(gx + below > 0)
     def _():
-        pl.semaphore_wait(barrier, gx * halves + below)
+        pl.semaphore_wait(barrier, gx * len(across) + below)
 
     greet(ready.at[gx], True)
 
@@ -222,7 +293,18 @@
         return acc
 
     load_vals.wait()
-    occ = contract(0, len(spans))
+    early = len(spans) // 2
+    occ = contract(0, early)
+    load_core.wait()
+    for a in range(gx_size):
+        cores[a] = core[:, a * points : (a + 1) * points]
+    for d in steps[::2]:
+
+        @pl.when(gx >= d)
+        def _():
+            lend(gx - d)
+
+    occ += contract(early, len(spans))
     occ = occ.astype(BF16)
     col_occ[own] = occ
     square = jnp.square(occ.astype(F32))
@@ -230,54 +312,72 @@
     low = (square - high.astype(F32)).astype(BF16)
     ones = jnp.ones((8, occ.shape[1]), BF16)
     dens[gx] = (dot(ones, high, 1, 1) + dot(ones, low, 1, 1))[:1]
-    for t in range(gx_size - 1):
-
-        @pl.when(gx > t)
-        def _():
-            dens_copy(t).start()
-            for k in range(halves):
-                row_copy(t, k).start()
-
 
     @pl.when(above > 0)
     def _():
         pl.semaphore_wait(ready.at[gx], above)
 
+    if halves > 1:
+        col_fwd(gy).start()
     for h in sides:
         col_copy(h).start()
-    if halves > 1:
-        col_fwd(gy).start()
+    for t in range(gx_size - 1):
+
+        @pl.when(gx > t)
+        def _():
+            dens_copy(t).start()
+
+        @pl.when((gx > t) & (lax.rem(jnp.abs(gx - t), 2) == 1))
+        def _():
+            for k in range(halves):
+                row_copy(t, k).start()
+
     for h in sides:
         col_win_copy(h).start()
     for h in range(gy_size):
         stage[h, :, :width] = vals[:, h * width : (h + 1) * width]
         if width < span:
             stage[h, :, width:] = jnp.zeros((points, span - width), BF16)
-    for h in sides:
-        cols_copy(h).start()
+    lead = part == halves - 1
+
+    @pl.when(lead)
+    def _():
+        for h in sides:
+            cols_copy(h).start()
+
     own_cols = pltpu.make_async_copy(stage.at[gy], cols.at[gy], load_sem.at[3])
     own_cols.start()
     for t in range(1, gx_size):
 
         @pl.when(gx < t)
         def _():
-            pl.semaphore_wait(ready.at[t], halves)
+            pl.semaphore_wait(ready.at[t], len(across))
             dens_copy(t).start()
+
+        @pl.when((gx < t) & (lax.rem(jnp.abs(gx - t), 2) == 0))
+        def _():
+            lend(t)
             for k in range(halves):
                 row_copy(t, k).start()
 
     for h, g in same:
         pl.semaphore_signal(known, inc=1, device_id=(gx, h, g), device_id_type=MESH)
     col_win[gy] = vals[:, :lanes]
-    load_core.wait()
     load_place.wait()
+    back[...] = jnp.zeros(back.shape, F32)
+    for z in range(gx_size):
+
+        @pl.when((gx != z) & jnp.logical_not(kept_by(z)))
+        def _():
+            tot_recv[pl.ds(z * crowd, crowd)] = jnp.zeros((crowd, *tot_recv.shape[1:]), BF16)
+
     spread = place[...]
     for k in range(halves):
 
         @pl.when(part == k)
         def _():
-            starts = [a * points + k * half for a in range(gx_size)]
-            core_q[...] = jnp.concatenate([core[:, s : s + half] for s in starts], axis=1)
+            for a in range(gx_size):
+                core_q[a] = core[:, a * points + k * half : a * points + (k + 1) * half]
 
     if sides:
         arrive(col_occ.at[pl.ds(0, len(sides))], col_sem)
@@ -305,47 +405,69 @@
         arrive(col_occ.at[pl.ds(0, gy_size)], col_sem, 1)
     for k in range(halves):
         row_occ[gx * halves + k] = col_occ[gy * halves + k, own_rows]
-    for z in planes:
-        arrive(row_occ.at[pl.ds(z * halves, halves)], row_sem, z)
-    gram = None
-    for k in range(halves):
-        row_vals = [row_occ[z * halves + k] for z in range(gx_size)]
-        col_vals = [col_occ[h * halves + k] for h in range(gy_size)]
-        row_vals, col_vals = (jnp.concatenate(v, axis=0) for v in (row_vals, col_vals))
-        term = dot(col_vals, row_vals, 1, 1)
-        gram = term if gram is None else gram + term
-    mixed = (core_q[...].astype(F32) * gram).astype(BF16)
-    block = dot(win_rows, mixed, 1, 0)
     tight = win_t.shape[1]
     layers = tight // 8
-    bands = []
-    for j in range(layers):
-        starts = [g * tight + j * 8 for g in range(gz_size)]
-        bands.append(jnp.concatenate([block[at : at + 8] for at in starts], axis=0))
-    for z in reversed(range(gx_size)):
-        pack = [band[:, z * half : (z + 1) * half] for band in bands]
+
+    def side_occ(k):
+        return jnp.concatenate([col_occ[h * halves + k] for h in range(gy_size)], axis=0)
+
+    def forward(z):
+        gram = None
+        for k in range(halves):
+            term = dot(side_occ(k), row_occ[z * halves + k], 1, 1)
+            gram = term if gram is None else gram + term
+        mixed = (core_q[z].astype(F32) * gram).astype(BF16)
+        block = dot(win_rows, mixed, 1, 0)
+        pack = []
+        for j in range(layers):
+            starts = [g * tight + j * 8 for g in range(gz_size)]
+            pack.append(jnp.concatenate([block[at : at + 8] for at in starts], axis=0))
         pack = jnp.concatenate(pack, axis=1).reshape(tot_send.shape[1:])
         tot_send[z] = pack.astype(BF16)
 
-        @pl.when(gx != z)
-        def _():
-            sweep(lambda i: tot_copy(z, *seat(i)).start())
-
-        @pl.when(gx == z)
-        def _():
-            for h, g in flat:
-                tot_copy(z, h, g).start()
-
+    def backward(z):
+        gram = None
+        for k in range(halves):
+            term = dot(row_occ[z * halves + k], side_occ(k), 1, 1)
+            gram = term if gram is None else gram + term
+        core_vals = jnp.concatenate([core_t[z, h].astype(F32) for h in range(gy_size)], axis=1)
+        mixed = (core_vals * gram).astype(BF16)
+        far_win = dot(spread, row_win[z], 0, 1).astype(BF16)
+        back[...] += dot(far_win, mixed, 1, 0)
+
+    forward(gx)
+    for h, g in flat:
+        tot_copy(gx, h, g).start()
     own_tot = pltpu.make_async_copy(
-        tot_send.at[gx, gz], tot_recv.at[gx * crowd + mine], tot_sem.at[1]
+        tot_send.at[gx, gz], tot_recv.at[gx * crowd + mine], tot_sem.at[1, gx]
     )
     own_tot.start()
+    for d in steps:
+        z = other(d)
+
+        @pl.when(inside(z))
+        def _():
+            lane_wait(row_occ.at[pl.ds(z * halves, halves)], row_sem, z)
+            lane_wait(row_win.at[z], row_win_sem, z)
+            lane_wait(core_t.at[z], core_sem, z)
+            forward(z)
+            sweep(lambda i: tot_copy(z, *seat(i)).start())
+            backward(z)
+
+    back_send[...] = back[...].reshape(back_send.shape).astype(BF16)
+    for h, g in flat:
+        back_copy(h, g).start()
+    own_back = pltpu.make_async_copy(back_send.at[gz], back_recv.at[mine], back_sem.at[1])
+    own_back.start()
 
     if sides:
-        arrive(cols.at[pl.ds(0, len(sides)), pl.ds(0, half)], cols_sem)
-    if halves > 1:
-        for h in sides:
-            cols_fwd(h).start()
+
+        @pl.when(lead)
+        def _():
+            arrive(cols.at[pl.ds(0, len(sides))], cols_sem)
+            if halves > 1:
+                for h in sides:
+                    cols_fwd(h).start()
 
     spare = 8 - rows
     reach = z_send.shape[3]
@@ -383,10 +505,20 @@
     weighted = (win_t[gz] * pot).astype(BF16).astype(F32)
     own_cols.wait()
     if halves > 1 and sides:
-        arrive(cols.at[pl.ds(0, len(sides)), pl.ds(0, half)], cols_sem, 1)
+
+        @pl.when(part == 0)
+        def _():
+            arrive(cols.at[pl.ds(0, len(sides))], cols_fwd_sem)
+
     spread_out(0, weighted)
 
-    arrive(tot_recv, tot_sem)
+    arrive(back_recv, back_sem)
+    for z in range(gx_size):
+
+        @pl.when((gx == z) | kept_by(z))
+        def _():
+            lane_wait(tot_recv.at[pl.ds(z * crowd, crowd)], tot_sem, z)
+
     total_of = []
     for i in range(gy_size * halves):
         h, k = divmod(i, halves)
@@ -401,17 +533,37 @@
         for j in range(layers)
     ]
     owned = jnp.concatenate(owned, axis=0)
+    owned += sum(back_recv[i].astype(F32) for i in range(crowd)).reshape(owned.shape)
     spread_out(1, owned)
 
     if sides:
         leave(col_win.at[pl.ds(0, len(sides))], col_win_sem)
-        leave(cols.at[pl.ds(0, len(sides))], cols_sem)
+
+        @pl.when(lead)
+        def _():
+            leave(cols.at[pl.ds(0, len(sides))], cols_sem)
+            if halves > 1:
+                leave(cols.at[pl.ds(0, len(sides))], cols_fwd_sem)
+
     if planes:
         leave(dens.at[pl.ds(0, len(planes))], dens_sem)
-        leave(row_occ.at[pl.ds(0, len(planes) * halves)], row_sem)
     leave(col_occ.at[pl.ds(0, len(sides) + gy_size * (halves - 1))], col_sem)
     leave(pot_recv.at[pl.ds(0, len(flat))], pot_sem)
-    leave(tot_recv.at[pl.ds(0, gx_size * crowd - 1)], tot_sem)
+    leave(back_recv.at[pl.ds(0, len(flat))], back_sem)
+    lane_leave(tot_recv.at[pl.ds(0, len(flat))], tot_sem, gx)
+    for d in steps:
+        t, z = keeper(d), other(d)
+
+        @pl.when(inside(t))
+        def _():
+            lane_leave(row_occ.at[pl.ds(0, halves)], row_sem, t)
+            lane_leave(row_win.at[0], row_win_sem, t)
+            lane_leave(core_t.at[0], core_sem, t)
+
+        @pl.when(inside(z))
+        def _():
+            lane_leave(tot_recv.at[pl.ds(0, crowd)], tot_sem, z)
+
 
     for index in range(2):
         if planes:
@@ -470,7 +622,11 @@
             vmem((total, occupied), BF16),
             vmem((row_count, flat), BF16),
             vmem(place.shape, BF16),
-            vmem((row_count, gx_size * half), BF16),
+            vmem((gx_size, row_count, half), BF16),
+            vmem((gx_size, row_count, points), BF16),
+            vmem((gx_size, gy_size, half, points), BF16),
+            vmem((gx_size, half, lanes), BF16),
+            vmem((gz_size * tight, side), F32),
             vmem((gx_size * halves, half, occupied), BF16),
             vmem((gy_size * halves, points, occupied), BF16),
             vmem((gy_size, points, lanes), BF16),
@@ -482,18 +638,24 @@
             vmem((gy_size * gz_size, 1, side), F32),
             vmem((gx_size, gz_size, 8, tight // 8 * half), BF16),
             vmem((gx_size * gy_size * gz_size, 8, tight // 8 * half), BF16),
+            vmem((gz_size, tight // 8, 8, side), BF16),
+            vmem((gy_size * gz_size, tight // 8, 8, side), BF16),
             vmem((2, gx_size, 8, reach), BF16),
             vmem((2, gx_size, 8, reach), BF16),
             dma((4,)),
             dma((-(-total // DEPTH),)),
             pltpu.SemaphoreType.REGULAR((gx_size,)),
             pltpu.SemaphoreType.REGULAR,
-            dma((1 + gx_size,)),
+            dma((2, gx_size)),
+            dma((2, gx_size)),
+            dma((2, gx_size)),
             dma((3,)),
             dma((2,)),
             dma((2,)),
-            dma((3,)),
             dma((2,)),
+            dma((2,)),
+            dma((2,)),
+            dma((2, gx_size)),
             dma((2,)),
             dma((3,)),
         ],

time: 23.9 us -> 24.1 us (level)
  no operation moved by 1% of the time
where the time goes in v2:
time: 24.1 us; the launch traced here: 23.9 us
  Pallas kernels  22.6 us (94%)
  local copies, waits for them, and re-layouts  0.66 us (3%)
  between operations  0.64 us (3%)
    pallas_call x1, Pallas kernels, local(): pl.pallas_call(functools.partial(kernel, dims), out_shape=pltpu.VMEM((2,...  22.6 us
    squeeze x1, local copies, waits for them, and re-layouts, local(): return (result[0], result[1])  0.66 us

profile of v2, /device:TPU:0, one launch (start us, length us, event | category | flops | bytes accessed | tf_op | source)
XLA Modules:
  0.0 23.9 jit_solution(7709044798126601895)
XLA Ops:
  0.6 22.6 %shard_map.59 = f32[2,6,2000]{2,1,0:T(8,128)S(1)} custom-call(bf16[96,4000]{1,0:T(8,128)(2,1)} %colloc_hbm.1, bf16[4000,256]{1,0:T(8,128)(2,1)} %coeffs_hbm.1, bf16[192,384]{1,0:T(8,128)(2,1)} %bitcast.5, bf16[128,96]{1,0:T(8,128)(2,1)} %constant.2.clone.place_hbm), custom_call_target="tpu_custom_call" | custom-call | tf_op jit(solution)/shard_map/pallas_call | solution.py:615
  23.3 0.7 %slice_bitcast_fusion = (f32[6,2000]{1,0:T(8,128)}, f32[6,2000]{1,0:T(8,128)}) fusion(f32[2,6,2000]{2,1,0:T(8,128)S(1)} %shard_map.59), kind=kLoop, calls=%fused_computation | loop fusion | bytes 192000 | tf_op jit(solution)/shard_map/squeeze | solution.py:666

commit v3 on v2

--- a/solution.py
+++ b/solution.py
@@ -41,7 +41,6 @@
     cores,
     core_t,
     row_win,
-    back,
     row_occ,
     col_occ,
     col_win,
@@ -172,6 +171,11 @@
     def inside(t):
         return (t >= 0) & (t < gx_size)
 
+    def keeps(z):
+        gap = z - gx
+        odd = lax.rem(jnp.abs(gap), 2)
+        return ((gap > 0) & (odd == 1)) | ((gap < 0) & (odd == 0))
+
     def kept_by(z):
         gap = gx - z
         odd = lax.rem(jnp.abs(gap), 2)
@@ -364,8 +368,16 @@
         pl.semaphore_signal(known, inc=1, device_id=(gx, h, g), device_id_type=MESH)
     col_win[gy] = vals[:, :lanes]
     load_place.wait()
-    back[...] = jnp.zeros(back.shape, F32)
     for z in range(gx_size):
+
+        @pl.when(jnp.logical_not(keeps(z)))
+        def _():
+            row_win[z] = jnp.zeros(row_win.shape[1:], BF16)
+            core_t[z] = jnp.zeros(core_t.shape[1:], BF16)
+
+        @pl.when((gx != z) & jnp.logical_not(keeps(z)))
+        def _():
+            row_occ[pl.ds(z * halves, halves)] = jnp.zeros((halves, *row_occ.shape[1:]), BF16)
 
         @pl.when((gx != z) & jnp.logical_not(kept_by(z)))
         def _():
@@ -376,14 +388,27 @@
 
         @pl.when(part == k)
         def _():
-            for a in range(gx_size):
-                core_q[a] = core[:, a * points + k * half : a * points + (k + 1) * half]
+            starts = [a * points + k * half for a in range(gx_size)]
+            core_q[...] = jnp.concatenate([core[:, s : s + half] for s in starts], axis=1)
 
     if sides:
         arrive(col_occ.at[pl.ds(0, len(sides))], col_sem)
     if halves > 1:
         for h in sides:
             col_fwd(h).start()
+    if sides:
+        arrive(col_win.at[pl.ds(0, len(sides))], col_win_sem)
+    wins = dot(spread, col_win[...].reshape(side, lanes), 0, 1)
+    win_t[...] = wins.reshape(win_t.shape)
+    win_rows = wins.astype(BF16)
+
+    if halves > 1:
+        arrive(col_occ.at[pl.ds(0, gy_size)], col_sem, 1)
+    for k in range(halves):
+        row_occ[gx * halves + k] = col_occ[gy * halves + k, own_rows]
+    tight = win_t.shape[1]
+    layers = tight // 8
+
     if planes:
         arrive(dens.at[pl.ds(0, len(planes))], dens_sem)
     density = jnp.concatenate([dens[z] for z in range(gx_size)], axis=1)
@@ -395,47 +420,35 @@
     for h, g in flat:
         pot_copy(h, g).start()
 
-    if sides:
-        arrive(col_win.at[pl.ds(0, len(sides))], col_win_sem)
-    wins = dot(spread, col_win[...].reshape(side, lanes), 0, 1)
-    win_t[...] = wins.reshape(win_t.shape)
-    win_rows = wins.astype(BF16)
-
-    if halves > 1:
-        arrive(col_occ.at[pl.ds(0, gy_size)], col_sem, 1)
-    for k in range(halves):
-        row_occ[gx * halves + k] = col_occ[gy * halves + k, own_rows]
-    tight = win_t.shape[1]
-    layers = tight // 8
-
     def side_occ(k):
         return jnp.concatenate([col_occ[h * halves + k] for h in range(gy_size)], axis=0)
 
-    def forward(z):
-        gram = None
-        for k in range(halves):
-            term = dot(side_occ(k), row_occ[z * halves + k], 1, 1)
-            gram = term if gram is None else gram + term
-        mixed = (core_q[z].astype(F32) * gram).astype(BF16)
-        block = dot(win_rows, mixed, 1, 0)
-        pack = []
-        for j in range(layers):
-            starts = [g * tight + j * 8 for g in range(gz_size)]
-            pack.append(jnp.concatenate([block[at : at + 8] for at in starts], axis=0))
+    def line_occ(k):
+        return jnp.concatenate([row_occ[z * halves + k] for z in range(gx_size)], axis=0)
+
+    for d in steps:
+        z = other(d)
+
+        @pl.when(inside(z))
+        def _():
+            lane_wait(row_occ.at[pl.ds(z * halves, halves)], row_sem, z)
+
+    gram = sum(dot(side_occ(k), line_occ(k), 1, 1) for k in range(halves))
+    mixed = (core_q[...].astype(F32) * gram).astype(BF16)
+    block = dot(win_rows, mixed, 1, 0)
+    bands = []
+    for j in range(layers):
+        starts = [g * tight + j * 8 for g in range(gz_size)]
+        bands.append(jnp.concatenate([block[at : at + 8] for at in starts], axis=0))
+    for z in reversed(range(gx_size)):
+        pack = [band[:, z * half : (z + 1) * half] for band in bands]
         pack = jnp.concatenate(pack, axis=1).reshape(tot_send.shape[1:])
         tot_send[z] = pack.astype(BF16)
 
-    def backward(z):
-        gram = None
-        for k in range(halves):
-            term = dot(row_occ[z * halves + k], side_occ(k), 1, 1)
-            gram = term if gram is None else gram + term
-        core_vals = jnp.concatenate([core_t[z, h].astype(F32) for h in range(gy_size)], axis=1)
-        mixed = (core_vals * gram).astype(BF16)
-        far_win = dot(spread, row_win[z], 0, 1).astype(BF16)
-        back[...] += dot(far_win, mixed, 1, 0)
-
-    forward(gx)
+        @pl.when(keeps(z))
+        def _():
+            sweep(lambda i: tot_copy(z, *seat(i)).start())
+
     for h, g in flat:
         tot_copy(gx, h, g).start()
     own_tot = pltpu.make_async_copy(
@@ -447,14 +460,17 @@
 
         @pl.when(inside(z))
         def _():
-            lane_wait(row_occ.at[pl.ds(z * halves, halves)], row_sem, z)
             lane_wait(row_win.at[z], row_win_sem, z)
             lane_wait(core_t.at[z], core_sem, z)
-            forward(z)
-            sweep(lambda i: tot_copy(z, *seat(i)).start())
-            backward(z)
-
-    back_send[...] = back[...].reshape(back_send.shape).astype(BF16)
+
+    core_vals = [
+        core_t[:, h].reshape(gx_size * half, points).astype(F32) for h in range(gy_size)
+    ]
+    far_win = dot(spread, row_win[...].reshape(-1, lanes), 0, 1).astype(BF16)
+    gram = sum(dot(line_occ(k), side_occ(k), 1, 1) for k in range(halves))
+    mixed = (jnp.concatenate(core_vals, axis=1) * gram).astype(BF16)
+    back = dot(far_win, mixed, 1, 0)
+    back_send[...] = back.reshape(back_send.shape).astype(BF16)
     for h, g in flat:
         back_copy(h, g).start()
     own_back = pltpu.make_async_copy(back_send.at[gz], back_recv.at[mine], back_sem.at[1])
@@ -622,11 +638,10 @@
             vmem((total, occupied), BF16),
             vmem((row_count, flat), BF16),
             vmem(place.shape, BF16),
-            vmem((gx_size, row_count, half), BF16),
+            vmem((row_count, gx_size * half), BF16),
             vmem((gx_size, row_count, points), BF16),
             vmem((gx_size, gy_size, half, points), BF16),
             vmem((gx_size, half, lanes), BF16),
-            vmem((gz_size * tight, side), F32),
             vmem((gx_size * halves, half, occupied), BF16),
             vmem((gy_size * halves, points, occupied), BF16),
             vmem((gy_size, points, lanes), BF16),

time: 24.1 us -> 23.2 us (0.963)
  Pallas kernels: 22.6 us -> 21.8 us
    pallas_call x1, Pallas kernels: 22.6 us -> 21.8 us  [local(): pl.pallas_call(functools.partial(kernel, dims), out_shape=pltpu.VMEM((2,...]
where the time goes in v3:
time: 23.2 us; the launch traced here: 23.1 us
  Pallas kernels  21.8 us (94%)
  local copies, waits for them, and re-layouts  0.66 us (3%)
  between operations  0.64 us (3%)
    pallas_call x1, Pallas kernels, local(): pl.pallas_call(functools.partial(kernel, dims), out_shape=pltpu.VMEM((2,...  21.8 us
    squeeze x1, local copies, waits for them, and re-layouts, local(): return (result[0], result[1])  0.66 us

profile of v3, /device:TPU:0, one launch (start us, length us, event | category | flops | bytes accessed | tf_op | source)
XLA Modules:
  0.0 23.1 jit_solution(12401912101980077876)
XLA Ops:
  0.6 21.8 %shard_map.59 = f32[2,6,2000]{2,1,0:T(8,128)S(1)} custom-call(bf16[96,4000]{1,0:T(8,128)(2,1)} %colloc_hbm.1, bf16[4000,256]{1,0:T(8,128)(2,1)} %coeffs_hbm.1, bf16[192,384]{1,0:T(8,128)(2,1)} %bitcast.5, bf16[128,96]{1,0:T(8,128)(2,1)} %constant.2.clone.place_hbm), custom_call_target="tpu_custom_call" | custom-call | tf_op jit(solution)/shard_map/pallas_call | solution.py:631
  22.4 0.7 %slice_bitcast_fusion = (f32[6,2000]{1,0:T(8,128)}, f32[6,2000]{1,0:T(8,128)}) fusion(f32[2,6,2000]{2,1,0:T(8,128)S(1)} %shard_map.59), kind=kLoop, calls=%fused_computation | loop fusion | bytes 192000 | tf_op jit(solution)/shard_map/squeeze | solution.py:681

commit v4 on v3

--- a/solution.py
+++ b/solution.py
@@ -213,7 +213,6 @@
         return lane_copy(src, row_win.at[gx], row_win_sem, t, (t, gy, gz))
 
     def lend(t):
-        row_win_copy(t).start()
         for h in range(gy_size):
             core_copy(t, h).start()
 
@@ -296,9 +295,6 @@
             acc += dot(vals[:, s : s + n], coeffs[s : s + n, :], 1, 0)
         return acc
 
-    load_vals.wait()
-    early = len(spans) // 2
-    occ = contract(0, early)
     load_core.wait()
     for a in range(gx_size):
         cores[a] = core[:, a * points : (a + 1) * points]
@@ -308,23 +304,30 @@
         def _():
             lend(gx - d)
 
-    occ += contract(early, len(spans))
+    load_vals.wait()
+    for d in steps[::2]:
+
+        @pl.when(gx >= d)
+        def _():
+            row_win_copy(gx - d).start()
+
+    occ = contract(0, len(spans))
     occ = occ.astype(BF16)
     col_occ[own] = occ
+    @pl.when(above > 0)
+    def _():
+        pl.semaphore_wait(ready.at[gx], above)
+
+    if halves > 1:
+        col_fwd(gy).start()
+    for h in sides:
+        col_copy(h).start()
     square = jnp.square(occ.astype(F32))
     high = square.astype(BF16)
     low = (square - high.astype(F32)).astype(BF16)
     ones = jnp.ones((8, occ.shape[1]), BF16)
     dens[gx] = (dot(ones, high, 1, 1) + dot(ones, low, 1, 1))[:1]
 
-    @pl.when(above > 0)
-    def _():
-        pl.semaphore_wait(ready.at[gx], above)
-
-    if halves > 1:
-        col_fwd(gy).start()
-    for h in sides:
-        col_copy(h).start()
     for t in range(gx_size - 1):
 
         @pl.when(gx > t)
@@ -361,6 +364,7 @@
         @pl.when((gx < t) & (lax.rem(jnp.abs(gx - t), 2) == 0))
         def _():
             lend(t)
+            row_win_copy(t).start()
             for k in range(halves):
                 row_copy(t, k).start()
 

time: 23.2 us -> 23.1 us (level)
  no operation moved by 1% of the time
where the time goes in v4:
time: 23.1 us; the launch traced here: 22.9 us
  Pallas kernels  21.6 us (94%)
  local copies, waits for them, and re-layouts  0.66 us (3%)
  between operations  0.64 us (3%)
    pallas_call x1, Pallas kernels, local(): pl.pallas_call(functools.partial(kernel, dims), out_shape=pltpu.VMEM((2,...  21.6 us
    squeeze x1, local copies, waits for them, and re-layouts, local(): return (result[0], result[1])  0.66 us

profile of v4, /device:TPU:0, one launch (start us, length us, event | category | flops | bytes accessed | tf_op | source)
XLA Modules:
  0.0 22.9 jit_solution(4967291270122808178)
XLA Ops:
  0.6 21.6 %shard_map.59 = f32[2,6,2000]{2,1,0:T(8,128)S(1)} custom-call(bf16[96,4000]{1,0:T(8,128)(2,1)} %colloc_hbm.1, bf16[4000,256]{1,0:T(8,128)(2,1)} %coeffs_hbm.1, bf16[192,384]{1,0:T(8,128)(2,1)} %bitcast.5, bf16[128,96]{1,0:T(8,128)(2,1)} %constant.2.clone.place_hbm), custom_call_target="tpu_custom_call" | custom-call | tf_op jit(solution)/shard_map/pallas_call | solution.py:635
  22.2 0.7 %slice_bitcast_fusion = (f32[6,2000]{1,0:T(8,128)}, f32[6,2000]{1,0:T(8,128)}) fusion(f32[2,6,2000]{2,1,0:T(8,128)S(1)} %shard_map.59), kind=kLoop, calls=%fused_computation | loop fusion | bytes 192000 | tf_op jit(solution)/shard_map/squeeze | solution.py:685

commit v5 on v4

--- a/solution.py
+++ b/solution.py
@@ -435,6 +435,16 @@
 
         @pl.when(inside(z))
         def _():
+            lane_wait(row_win.at[z], row_win_sem, z)
+            lane_wait(core_t.at[z], core_sem, z)
+
+    far_win = dot(spread, row_win[...].reshape(-1, lanes), 0, 1).astype(BF16)
+
+    for d in steps:
+        z = other(d)
+
+        @pl.when(inside(z))
+        def _():
             lane_wait(row_occ.at[pl.ds(z * halves, halves)], row_sem, z)
 
     gram = sum(dot(side_occ(k), line_occ(k), 1, 1) for k in range(halves))
@@ -459,18 +469,9 @@
         tot_send.at[gx, gz], tot_recv.at[gx * crowd + mine], tot_sem.at[1, gx]
     )
     own_tot.start()
-    for d in steps:
-        z = other(d)
-
-        @pl.when(inside(z))
-        def _():
-            lane_wait(row_win.at[z], row_win_sem, z)
-            lane_wait(core_t.at[z], core_sem, z)
-
     core_vals = [
         core_t[:, h].reshape(gx_size * half, points).astype(F32) for h in range(gy_size)
     ]
-    far_win = dot(spread, row_win[...].reshape(-1, lanes), 0, 1).astype(BF16)
     gram = sum(dot(line_occ(k), side_occ(k), 1, 1) for k in range(halves))
     mixed = (jnp.concatenate(core_vals, axis=1) * gram).astype(BF16)
     back = dot(far_win, mixed, 1, 0)

time: 23.1 us -> 23.1 us (level)
  no operation moved by 1% of the time
where the time goes in v5:
time: 23.1 us; the launch traced here: 23 us
  Pallas kernels  21.7 us (94%)
  local copies, waits for them, and re-layouts  0.66 us (3%)
  between operations  0.64 us (3%)
    pallas_call x1, Pallas kernels, local(): pl.pallas_call(functools.partial(kernel, dims), out_shape=pltpu.VMEM((2,...  21.7 us
    squeeze x1, local copies, waits for them, and re-layouts, local(): return (result[0], result[1])  0.66 us

profile of v5, /device:TPU:0, one launch (start us, length us, event | category | flops | bytes accessed | tf_op | source)
XLA Modules:
  0.0 23.0 jit_solution(10107320562950632469)
XLA Ops:
  0.6 21.7 %shard_map.59 = f32[2,6,2000]{2,1,0:T(8,128)S(1)} custom-call(bf16[96,4000]{1,0:T(8,128)(2,1)} %colloc_hbm.1, bf16[4000,256]{1,0:T(8,128)(2,1)} %coeffs_hbm.1, bf16[192,384]{1,0:T(8,128)(2,1)} %bitcast.5, bf16[128,96]{1,0:T(8,128)(2,1)} %constant.2.clone.place_hbm), custom_call_target="tpu_custom_call" | custom-call | tf_op jit(solution)/shard_map/pallas_call | solution.py:636
  22.3 0.7 %slice_bitcast_fusion = (f32[6,2000]{1,0:T(8,128)}, f32[6,2000]{1,0:T(8,128)}) fusion(f32[2,6,2000]{2,1,0:T(8,128)S(1)} %shard_map.59), kind=kLoop, calls=%fused_computation | loop fusion | bytes 192000 | tf_op jit(solution)/shard_map/squeeze | solution.py:686
